TPU v7x, 256 devices: a whole 4x4x8 slice. The times are simulated.
256 devices in a mesh: vert: 256 (over z, x, y, core).
Axes of the slice: x: 4, y: 4, z: 8, core: 2. Of those that a mesh axis runs over, the one named last changes fastest.
Arguments:
- feats: bfloat16 [524288, 128], P('vert'), may hold values from -6 to 6
- w_self: bfloat16 [128, 256], replicated, may hold values from -0.5 to 0.5
- w_neigh: bfloat16 [128, 256], replicated, may hold values from -0.5 to 0.5
- bias: float32 [256], replicated, may hold values from -0.6 to 0.6
- cotangent: bfloat16 [524288, 256], P('vert'), may hold values from -24 to 24
- send_rows: int32 [256, 256, 8], P('vert'), may hold values from 0 to 2047
- hub_ids: int32 [368], replicated, may hold values from 0 to 524287, as said below
- edge_src: int32 [256, 16384], P('vert'), may hold values from 0 to 4463, as said below
- edge_dst: int32 [256, 16384], P('vert'), may hold values from 0 to 2047, never falling along the last dimension, each value on 1 to 64 neighbouring positions
- edge_count: int32 [256], P('vert'), may hold values from 1 to 16384, 1677721 in all
Outputs:
- output: bfloat16 [524288, 256], P('vert')
- grad_feats: bfloat16 [524288, 128], P('vert')
- grad_w_self: float32 [128, 256], replicated
- grad_w_neigh: float32 [128, 256], replicated
- grad_bias: float32 [256], replicated
Inputs may be any that keep to these rules, and one draw needn't show every extreme that they name: edge_src[d, e] indexes block d's source table: values below 2048 are own rows, values from 2048 to 4095 are halo slots (owner p = (value - 2048) // 8, slot c = (value - 2048) % 8), higher values are hubs (index value - 2048 - 256*8 into hub_ids). hub_ids is strictly ascending; no device's id range holds more than 8 hubs, some device's range holds exactly 8, and every device's range holds at least one.
All inputs are finite; a program needn't handle non-finite values.
Results may differ from a plain program's by a relative error of at most 0.0055.
Values may be sent and summed in bfloat16 or wider, within the bound.
No kernel may reach another device: no remote copies, remote signals or barrier semaphores. Data moves between devices by JAX's collectives and lax.ppermute only.
A program may use at most 64 MiB of HBM per device.

v0:
```python
import jax
import jax.numpy as jnp
from jax import lax
from jax.experimental import pallas as pl
from jax.experimental.pallas import tpu as pltpu
from jax.sharding import PartitionSpec as P


CHUNK = 256
WINDOW = 128
ACCS = 8
ITEMS = 4
HUB_MOST = 8
BF16 = jnp.bfloat16
F32 = jnp.float32

SMEM = pl.BlockSpec(memory_space=pltpu.SMEM)
VMEM = pl.BlockSpec(memory_space=pltpu.VMEM)


def first_hub(ids_ref, floor):
    total = ids_ref.shape[0]
    low, high = jnp.int32(0), jnp.int32(total)
    for _ in range(total.bit_length()):
        middle = jnp.minimum((low + high) // 2, total - 1)
        below = jnp.logical_and(low < high, ids_ref[middle] < floor)
        above = jnp.logical_and(low < high, jnp.logical_not(below))
        low = jnp.where(below, middle + 1, low)
        high = jnp.where(above, middle, high)
    return low


def own_hub(ids_ref, first, floor, local_rows, i):
    at = jnp.minimum(first + i, ids_ref.shape[0] - 1)
    local = ids_ref[at] - floor
    held = jnp.logical_and(first + i < ids_ref.shape[0], local < local_rows)
    return held, jnp.where(held, local, 0)


def pack_kernel(own_ref, ids_ref, rows_ref, feats_ref, send_ref, table, picked):
    local_rows, width = feats_ref.shape
    peers, depth, _ = send_ref.shape
    slots = rows_ref.shape[0] // peers
    group = CHUNK // slots
    most = depth - slots
    table[...] = feats_ref[...].astype(F32)
    floor = own_ref[0] * local_rows
    first = first_hub(ids_ref, floor)
    for i in range(most):
        _, local = own_hub(ids_ref, first, floor, local_rows, i)
        picked[pl.ds(i, 1), :] = table[pl.ds(local, 1), :]
    hubs = jnp.broadcast_to(picked[0:most, :][None], (group, most, width))

    def chunk(c, carry):
        for e in range(CHUNK):
            picked[pl.ds(e, 1), :] = table[pl.ds(rows_ref[c * CHUNK + e], 1), :]
        halo = picked[...].reshape(group, slots, width)
        both = jnp.concatenate([halo, hubs], axis=1)
        send_ref[pl.ds(c * group, group), :, :] = both.astype(BF16)
        return carry

    lax.fori_loop(0, rows_ref.shape[0] // CHUNK, chunk, 0)


def layer_kernel(
    count_ref, starts_ref, src_ref, ids_ref, dst_ref, feats_ref, come_ref, cot_ref, self_ref,
    neigh_ref, bias_ref, out_ref, own_ref, send_ref, table, come, picked_a, picked_b, sums, spread,
    weights_ref, wgrad, parts, *accs,
):
    local_rows, width = feats_ref.shape
    wide = self_ref.shape[1]
    peers, depth, _ = come_ref.shape
    slots = depth - HUB_MOST
    halo_rows = peers * slots
    hub_total = ids_ref.shape[0]
    hub_base = local_rows + halo_rows
    last_chunk = dst_ref.shape[1] // CHUNK - 1
    count = count_ref[0]
    pairs = (count + (2 * CHUNK - 1)) // (2 * CHUNK)

    table[0:local_rows, :] = feats_ref[...].astype(F32)
    come[...] = come_ref[...].astype(F32).reshape(peers * depth, width)
    table[local_rows:hub_base, :] = (
        come[...].reshape(peers, depth, width)[:, 0:slots, :].reshape(halo_rows, width)
    )
    before, offset = jnp.int32(-1), jnp.int32(0)
    for h in range(hub_total):
        owner = ids_ref[h] // local_rows
        offset = jnp.where(owner == before, offset + 1, 0)
        before = owner
        table[pl.ds(hub_base + h, 1), :] = come[pl.ds(owner * depth + slots + offset, 1), :]
    sums[...] = jnp.zeros_like(sums)

    edge_lane = lax.broadcasted_iota(jnp.int32, (1, CHUNK), 1)
    row_id = lax.broadcasted_iota(jnp.int32, (WINDOW, CHUNK), 0)

    def window_of(c):
        low = (starts_ref[0, c] // 16) * 16
        until = starts_ref[0, jnp.minimum(c + 1, last_chunk)]
        until = jnp.where(c < last_chunk, until, local_rows - 1)
        return low, (until - low) // WINDOW + 1

    def targets(c):
        row = dst_ref[:, pl.ds(pl.multiple_of(c * CHUNK, CHUNK), CHUNK)]
        return jnp.where(edge_lane + c * CHUNK < count, row, -1)

    def one_hot(row, at):
        return jnp.where(row_id + at == row, 1.0, 0.0).astype(BF16)

    def gather(c, into):
        for e in range(CHUNK):
            into[pl.ds(e, 1), :] = table[pl.ds(src_ref[c * CHUNK + e], 1), :]

    def add_up(c, held):
        low, blocks = window_of(c)
        row = targets(c)
        rhs = jnp.concatenate([held[...].astype(BF16), jnp.ones((CHUNK, width), BF16)], axis=1)

        def block(i):
            at = pl.multiple_of(low + i * WINDOW, 16)
            sums[pl.ds(at, WINDOW), :] += jnp.dot(one_hot(row, at), rhs, preferred_element_type=F32)

        block(0)

        def more():
            def step(i, inner):
                block(i)
                return inner

            lax.fori_loop(1, blocks, step, 0)

        return more

    def forward(p, carry):
        for half, held, ahead in ((0, picked_a, picked_b), (1, picked_b, picked_a)):
            c = 2 * p + half
            gather(jnp.minimum(c + 1, last_chunk), ahead)
            add_up(c, held)()
        return carry

    gather(0, picked_a)
    lax.fori_loop(0, pairs, forward, 0)

    wgrad[...] = jnp.zeros_like(wgrad)
    parts[...] = jnp.zeros_like(parts)
    spread[pl.ds(local_rows, WINDOW), :] = jnp.zeros((WINDOW, width), BF16)
    weights_ref[0:width, :] = self_ref[...]
    weights_ref[width:, :] = neigh_ref[...]
    bias = bias_ref[...]

    def dense(b, bias_sum):
        at = pl.multiple_of(b * CHUNK, CHUNK)
        weights = weights_ref[...]
        inverse = 1.0 / jnp.maximum(sums[pl.ds(at, CHUNK), width:], 1.0)
        mean = (sums[pl.ds(at, CHUNK), :width] * inverse).astype(BF16)
        both = jnp.concatenate([feats_ref[pl.ds(at, CHUNK), :], mean], axis=1)
        linear = jnp.dot(both, weights, preferred_element_type=F32) + bias
        logistic = jax.nn.sigmoid(linear)
        out_ref[pl.ds(at, CHUNK), :] = (linear * logistic).astype(BF16)
        slope = logistic * (1.0 + linear * (1.0 - logistic))
        grad = (cot_ref[pl.ds(at, CHUNK), :].astype(F32) * slope).astype(BF16)
        wgrad[...] += lax.dot_general(both, grad, (((0,), (0,)), ((), ())), preferred_element_type=F32)
        back = lax.dot_general(grad, weights, (((1,), (1,)), ((), ())), preferred_element_type=F32)
        own_ref[pl.ds(at, CHUNK), :] = back[:, :width]
        spread[pl.ds(at, CHUNK), :] = (back[:, width:] * inverse).astype(BF16)
        return bias_sum + jnp.sum(grad.astype(F32), axis=0, keepdims=True)

    bias_sum = lax.fori_loop(0, local_rows // CHUNK, dense, jnp.zeros((1, wide), F32))

    for acc in accs:
        acc[...] = jnp.zeros_like(acc)

    def expand(c, into):
        low, blocks = window_of(c)
        row = targets(c)

        def block(i):
            at = pl.multiple_of(low + i * WINDOW, 16)
            return lax.dot_general(
                one_hot(row, at), spread[pl.ds(at, WINDOW), :], (((0,), (0,)), ((), ())),
                preferred_element_type=F32,
            )

        into[...] = block(0)

        def more():
            def step(i, inner):
                into[...] += block(i)
                return inner

            lax.fori_loop(1, blocks, step, 0)

        return more

    def scatter(c, held):
        for e in range(0, CHUNK, ACCS):
            to = [src_ref[c * CHUNK + e + k] for k in range(ACCS)]
            new = [accs[k][pl.ds(to[k], 1), :] + held[pl.ds(e + k, 1), :] for k in range(ACCS)]
            for k in range(ACCS):
                accs[k][pl.ds(to[k], 1), :] = new[k]

    def backward(p, carry):
        for half, held, ahead in ((0, picked_a, picked_b), (1, picked_b, picked_a)):
            c = 2 * p + half
            scatter(c, held)
            expand(jnp.minimum(c + 1, last_chunk), ahead)()
        return carry

    expand(0, picked_a)()
    lax.fori_loop(0, pairs, backward, 0)

    def total(at, size):
        value = accs[0][pl.ds(at, size), :]
        for acc in accs[1:]:
            value = value + acc[pl.ds(at, size), :]
        return value

    def fold(b, carry):
        at = pl.multiple_of(b * CHUNK, CHUNK)
        own_ref[pl.ds(at, CHUNK), :] += total(at, CHUNK)
        return carry

    lax.fori_loop(0, local_rows // CHUNK, fold, 0)
    group = CHUNK // slots

    wide_rows = 2 * width
    parts[0:wide_rows, :] = wgrad[:, :width]
    parts[wide_rows : 2 * wide_rows, :] = wgrad[:, width:]
    parts[pl.ds(2 * wide_rows, 1), :] = bias_sum[:, :width]
    parts[pl.ds(2 * wide_rows + 1, 1), :] = bias_sum[:, width:]
    parts[2 * wide_rows + 8 : 2 * wide_rows + 8 + hub_total, :] = total(hub_base, hub_total)
    for j in range(ITEMS):
        item = parts[j * peers : (j + 1) * peers, :]
        high = item.astype(BF16).astype(F32)
        table[pl.ds(j, peers, stride=2 * ITEMS), :] = high
        table[pl.ds(j + ITEMS, peers, stride=2 * ITEMS), :] = item - high

    def emit(b, carry):
        at = pl.multiple_of(b * CHUNK, CHUNK)
        halo = total(pl.multiple_of(local_rows + at, CHUNK), CHUNK).reshape(group, slots, width)
        items = table[pl.ds(at, CHUNK), :].reshape(group, 2 * ITEMS, width)
        send_ref[pl.ds(b * group, group), :, :] = jnp.concatenate([halo, items], axis=1).astype(BF16)
        return carry

    lax.fori_loop(0, halo_rows // CHUNK, emit, 0)


def finish_kernel(
    floor_ref, shifted_ref, ids_ref, rows_ref, own_ref, back_ref, items_ref, grad_ref, self_ref, neigh_ref,
    bias_ref, rows_in, *accs,
):
    local_rows, width = own_ref.shape
    peers, _, _ = back_ref.shape
    slots = rows_ref.shape[0] // peers
    half = self_ref.shape[0]
    accs[0][...] = own_ref[...]
    for acc in accs[1:]:
        acc[...] = jnp.zeros_like(acc)
    rows_in[...] = back_ref[:, 0:slots, :].astype(F32).reshape(peers * slots, width)

    def chunk(c, carry):
        at = c * CHUNK
        for e in range(0, CHUNK, ACCS):
            to = [rows_ref[at + e + k] for k in range(ACCS)]
            new = [
                accs[k][pl.ds(to[k], 1), :] + rows_in[pl.ds(at + e + k, 1), :]
                for k in range(ACCS)
            ]
            for k in range(ACCS):
                accs[k][pl.ds(to[k], 1), :] = new[k]
        return carry

    lax.fori_loop(0, rows_ref.shape[0] // CHUNK, chunk, 0)
    floor = floor_ref[0]
    first = first_hub(shifted_ref, 0)
    for i in range(HUB_MOST):
        held, to = own_hub(ids_ref, first, floor, local_rows, i)
        item = jnp.where(held, 4 * half + 8 + first + i, 0)
        row = items_ref[pl.ds((item % peers) * ITEMS + item // peers, 1), :]
        row = jnp.where(held, row, 0.0)
        accs[0][pl.ds(to, 1), :] += row

    def fold(b, carry):
        at = pl.multiple_of(b * CHUNK, CHUNK)
        value = accs[0][pl.ds(at, CHUNK), :]
        for acc in accs[1:]:
            value = value + acc[pl.ds(at, CHUNK), :]
        grad_ref[pl.ds(at, CHUNK), :] = value.astype(BF16)
        return carry

    lax.fori_loop(0, local_rows // CHUNK, fold, 0)
    for j in range(2):
        item = items_ref[pl.ds(j, peers, stride=ITEMS), :]
        self_ref[:, j * width : (j + 1) * width] = item[:half]
        neigh_ref[:, j * width : (j + 1) * width] = item[half:]
    for j in range(2):
        bias_ref[:, j * width : (j + 1) * width] = items_ref[pl.ds(j * ITEMS + 2, 1), :]


def exchange(array):
    return lax.all_to_all(array, "vert", split_axis=0, concat_axis=0, tiled=True)


def body(
    feats, w_self, w_neigh, bias, cotangent, send_rows, hub_ids, edge_src, edge_dst, edge_count
):
    local_rows, width = feats.shape
    wide = w_self.shape[1]
    peers = lax.axis_size("vert")
    slots = send_rows.shape[2]
    hubs = hub_ids.shape[0]
    edges = edge_src.shape[1]
    halo_rows = peers * slots
    table_rows = -(-(local_rows + halo_rows + hubs) // 16) * 16
    own = lax.axis_index("vert").astype(jnp.int32).reshape(1)
    rows = send_rows.reshape(halo_rows)

    sent = pl.pallas_call(
        pack_kernel,
        out_shape=jax.ShapeDtypeStruct((peers, slots + HUB_MOST, width), BF16),
        in_specs=[SMEM, SMEM, SMEM, VMEM],
        out_specs=VMEM,
        scratch_shapes=[pltpu.VMEM((local_rows, width), F32), pltpu.VMEM((CHUNK, width), F32)],
        name="pack",
    )(own, hub_ids, rows, feats)
    come = exchange(sent)

    starts = edge_dst[:, ::CHUNK]
    output, own_grad, outgoing = pl.pallas_call(
        layer_kernel,
        out_shape=(
            jax.ShapeDtypeStruct((local_rows, wide), BF16),
            jax.ShapeDtypeStruct((local_rows, width), F32),
            jax.ShapeDtypeStruct((peers, slots + 2 * ITEMS, width), BF16),
        ),
        in_specs=[SMEM, SMEM, SMEM, SMEM] + [VMEM] * 7,
        out_specs=(VMEM, VMEM, VMEM),
        scratch_shapes=[
            pltpu.VMEM((table_rows, width), F32),
            pltpu.VMEM((peers * (slots + HUB_MOST), width), F32),
            pltpu.VMEM((CHUNK, width), F32),
            pltpu.VMEM((CHUNK, width), F32),
            pltpu.VMEM((local_rows + 4 * WINDOW, 2 * width), F32),
            pltpu.VMEM((local_rows + WINDOW, width), BF16),
            pltpu.VMEM((2 * width, wide), BF16),
            pltpu.VMEM((2 * width, wide), F32),
            pltpu.VMEM((ITEMS * peers, width), F32),
        ]
        + [pltpu.VMEM((table_rows, width), F32)] * ACCS,
        compiler_params=pltpu.CompilerParams(vmem_limit_bytes=56 * 1024 * 1024),
        name="layer",
    )(
        edge_count, starts, edge_src.reshape(edges), hub_ids, edge_dst, feats, come, cotangent,
        w_self, w_neigh, bias.reshape(1, wide),
    )
    back = exchange(outgoing)
    hubs_a = hub_ids - own * local_rows
    floors = lax.iota(jnp.int32, 8) + own * local_rows
    summed = jnp.sum(back[:, slots:].astype(F32), axis=0)
    items = (summed[:ITEMS] + summed[ITEMS:])[None]
    items = exchange(jnp.broadcast_to(items, (peers, ITEMS, width)))
    grad_feats, grad_self, grad_neigh, grad_bias = pl.pallas_call(
        finish_kernel,
        out_shape=(
            jax.ShapeDtypeStruct((local_rows, width), BF16),
            jax.ShapeDtypeStruct((width, wide), F32),
            jax.ShapeDtypeStruct((width, wide), F32),
            jax.ShapeDtypeStruct((1, wide), F32),
        ),
        in_specs=[SMEM, SMEM, SMEM, SMEM] + [VMEM] * 3,
        out_specs=(VMEM,) * 4,
        scratch_shapes=[pltpu.VMEM((halo_rows, width), F32)]
        + [pltpu.VMEM((local_rows, width), F32)] * ACCS,
        name="finish",
    )(floors, hubs_a, hub_ids, rows, own_grad, back, items.reshape(peers * ITEMS, width))
    return (output, grad_feats, grad_self, grad_neigh, grad_bias.reshape(wide))


def solution(mesh):
    in_specs = (
        P("vert", None),
        P(),
        P(),
        P(),
        P("vert", None),
        P("vert", None, None),
        P(),
        P("vert", None),
        P("vert", None),
        P("vert"),
    )
    out_specs = (P("vert", None), P("vert", None), P(), P(), P())
    return jax.shard_map(body, mesh=mesh, in_specs=in_specs, out_specs=out_specs, check_vma=False)
```

profile of v0, /device:TPU:2, one launch (start us, length us, event | category | flops | bytes accessed | tf_op | source)
XLA Modules:
  0.0 179.7 jit_solution(3529964805296197285)
XLA Ops:
  0.6 0.8 copy.15
  1.5 0.7 reshape.31.rows_ref
  2.2 3.9 %pack.1 = bf16[256,16,128]{2,1,0:T(8,128)(2,1)} custom-call(s32[1]{0:T(128)} %bitcast.1.own_ref, s32[368]{0:T(512)} %ids_ref.5, s32[2048]{0:T(1024)} %reshape.31.rows_ref, bf16[2048,128]{1,0:T(8,128)(2,1)} %feats_ref.3), custom_call_target="tpu_custom_call" | custom-call | tf_op jit(solution)/shard_map/pack/pallas_call | solution.py:318
  6.1 14.7 %all-to-all-start = ((bf16[256,16,128]{2,1,0:T(8,128)(2,1)}), bf16[256,16,128]{2,1,0:T(8,128)(2,1)S(1)}, u32[]{:S(2)}, u32[]{:S(2)}) async-start(bf16[256,16,128]{2,1,0:T(8,128)(2,1)} %pack.1), calls=%async_computation | async-start | bytes 2097152 | tf_op jit(solution)/shard_map/all_to_all | solution.py:301
  21.5 1.5 slice.12.starts_ref
  23.0 29.1 %all-to-all-done.come_ref = bf16[256,16,128]{2,1,0:T(8,128)(2,1)S(1)} async-done(((bf16[256,16,128]{2,1,0:T(8,128)(2,1)}), bf16[256,16,128]{2,1,0:T(8,128)(2,1)S(1)}, u32[]{:S(2)}, u32[]{:S(2)}) %all-to-all-start) | async-done | bytes 1048608 | tf_op jit(solution)/shard_map/all_to_all | solution.py:301
  52.1 0.0 copy-start.1
  52.1 1.0 copy-done.1
  53.1 18.8 %layer.1 = (bf16[2048,256]{1,0:T(8,128)(2,1)}, f32[2048,128]{1,0:T(8,128)}, bf16[256,16,128]{2,1,0:T(8,128)(2,1)}) custom-call(s32[1]{0:T(128)S(6)} %copy.16.count_ref, s32[1,64]{1,0:T(1,128)} %slice.12.starts_ref, s32[16384]{0:T(1024)} %bitcast.7, s32[368]{0:T(512)} %ids_ref.5, s32[1,16384]{1,0:T(1,128)} %dst_ref.1, bf16[2048,128]{1,0:T(8,128)(2,1)} %feats_ref.3, ...), custom_call_target="tpu_custom_call" | custom-call | tf_op jit(solution)/shard_map/layer/pallas_call | solution.py:329
  71.9 74.5 %all_to_all.15.back_ref = bf16[256,16,128]{2,1,0:T(8,128)(2,1)S(1)} all-to-all(bf16[256,16,128]{2,1,0:T(8,128)(2,1)} %get-tuple-element.14), channel_id=1, replica_groups=mesh['vert'=256] {'vert'}, dimensions={0} | all-to-all | bytes 2097152 | tf_op jit(solution)/shard_map/all_to_all | solution.py:301
  146.4 0.0 copy-start
  146.4 0.3 convert_reduce_fusion
  146.7 0.9 broadcast_in_dim.2
  147.6 0.0 copy-done
  147.6 5.7 %all-to-all-start.2 = ((f32[256,4,128]{2,1,0:T(4,128)}), f32[256,4,128]{2,1,0:T(4,128)S(1)}, u32[]{:S(2)}, u32[]{:S(2)}) async-start(f32[256,4,128]{2,1,0:T(4,128)} %broadcast_in_dim.2), calls=%async_computation.2 | async-start | bytes 1048576 | tf_op jit(solution)/shard_map/all_to_all | solution.py:301
  153.3 0.0 copy-start.3
  153.3 0.5 iota_add_fusion.floor_ref
  153.9 0.2 copy-done.3
  154.0 0.6 broadcast_subtract_fusion.shifted_ref
  154.6 18.9 %all-to-all-done.2 = f32[256,4,128]{2,1,0:T(4,128)S(1)} async-done(((f32[256,4,128]{2,1,0:T(4,128)}), f32[256,4,128]{2,1,0:T(4,128)S(1)}, u32[]{:S(2)}, u32[]{:S(2)}) %all-to-all-start.2) | async-done | bytes 524320 | tf_op jit(solution)/shard_map/all_to_all | solution.py:301
  173.5 0.0 copy-start.2
  173.5 0.8 copy-done.2
  174.3 5.5 %finish.1 = (bf16[2048,128]{1,0:T(8,128)(2,1)}, f32[128,256]{1,0:T(8,128)}, f32[128,256]{1,0:T(8,128)}, f32[1,256]{1,0:T(1,128)}) custom-call(s32[8]{0:T(128)} %iota_add_fusion.floor_ref, s32[368]{0:T(512)} %broadcast_subtract_fusion.shifted_ref, s32[368]{0:T(512)} %ids_ref.5, s32[2048]{0:T(1024)} %reshape.31.rows_ref, ...), custom_call_target="tpu_custom_call" | custom-call | tf_op jit(solution)/shard_map/finish/pallas_call | solution.py:362
  (1 shorter events, 0.0 us)
Async XLA Ops:
  6.1 46.0 %all-to-all-start = ((bf16[256,16,128]{2,1,0:T(8,128)(2,1)}), bf16[256,16,128]{2,1,0:T(8,128)(2,1)S(1)}, u32[]{:S(2)}, u32[]{:S(2)}) async-start(bf16[256,16,128]{2,1,0:T(8,128)(2,1)} %pack.1), calls=%async_computation | async-start | bytes 2097152 | tf_op jit(solution)/shard_map/all_to_all | solution.py:301
  52.1 1.0 copy-start.1
  146.4 1.2 copy-start
  147.6 25.9 %all-to-all-start.2 = ((f32[256,4,128]{2,1,0:T(4,128)}), f32[256,4,128]{2,1,0:T(4,128)S(1)}, u32[]{:S(2)}, u32[]{:S(2)}) async-start(f32[256,4,128]{2,1,0:T(4,128)} %broadcast_in_dim.2), calls=%async_computation.2 | async-start | bytes 1048576 | tf_op jit(solution)/shard_map/all_to_all | solution.py:301
  153.3 0.7 copy-start.3
  173.5 0.8 copy-start.2
where the time goes:
time: 181 us; the launch traced here: 180 us
  blocking collectives  74.5 us (41%)
  waiting for transfers between devices  48 us (27%)
  Pallas kernels  28.2 us (16%)
  starting transfers between devices  20.4 us (11%)
  local copies, waits for them, and re-layouts  5.93 us (3%)
    all_to_all x1, blocking collectives, exchange(): lax.all_to_all(array, 'vert', split_axis=0, concat_axis=0, tiled=True)  74.5 us
    all_to_all x2, waiting for transfers between devices, exchange(): lax.all_to_all(array, 'vert', split_axis=0, concat_axis=0, tiled=True)  48 us
    all_to_all x2, starting transfers between devices, exchange(): lax.all_to_all(array, 'vert', split_axis=0, concat_axis=0, tiled=True)  20.4 us
    pallas_call x1, Pallas kernels, body(): pl.pallas_call(layer_kernel, out_shape=(jax.ShapeDtypeStruct((local_rows,...  18.8 us
    pallas_call x1, Pallas kernels, body(): pl.pallas_call(finish_kernel, out_shape=(jax.ShapeDtypeStruct((local_rows...  5.47 us
    pallas_call x1, Pallas kernels, body(): pl.pallas_call(pack_kernel, out_shape=jax.ShapeDtypeStruct((peers, slots...  3.94 us
  transfers between devices with their start and end apart: 2, of which 2 were waited for; matrix products, arithmetic and copies ran while one was open for 1% of the time, Pallas kernels for 0%

commit v1 on v0

v1 whole, which is shorter than its diff:
```python
import jax
import jax.numpy as jnp
from jax import lax
from jax.experimental import pallas as pl
from jax.experimental.pallas import tpu as pltpu
from jax.sharding import PartitionSpec as P


CHUNK = 256
WINDOW = 128
ACCS = 8
HUB_MOST = 8
BF16 = jnp.bfloat16
F32 = jnp.float32

SMEM = pl.BlockSpec(memory_space=pltpu.SMEM)
VMEM = pl.BlockSpec(memory_space=pltpu.VMEM)


def first_hub(ids_ref, floor):
    total = ids_ref.shape[0]
    low, high = jnp.int32(0), jnp.int32(total)
    for _ in range(total.bit_length()):
        middle = jnp.minimum((low + high) // 2, total - 1)
        below = jnp.logical_and(low < high, ids_ref[middle] < floor)
        above = jnp.logical_and(low < high, jnp.logical_not(below))
        low = jnp.where(below, middle + 1, low)
        high = jnp.where(above, middle, high)
    return low


def own_hub(ids_ref, first, floor, local_rows, i):
    at = jnp.minimum(first + i, ids_ref.shape[0] - 1)
    local = ids_ref[at] - floor
    held = jnp.logical_and(first + i < ids_ref.shape[0], local < local_rows)
    return held, jnp.where(held, local, 0)


def pack_kernel(own_ref, ids_ref, rows_ref, feats_ref, send_ref, table, picked):
    local_rows, width = feats_ref.shape
    peers, depth, _ = send_ref.shape
    slots = rows_ref.shape[0] // peers
    group = CHUNK // slots
    most = depth - slots
    table[...] = feats_ref[...].astype(F32)
    floor = own_ref[0] * local_rows
    first = first_hub(ids_ref, floor)
    for i in range(most):
        _, local = own_hub(ids_ref, first, floor, local_rows, i)
        picked[pl.ds(i, 1), :] = table[pl.ds(local, 1), :]
    hubs = jnp.broadcast_to(picked[0:most, :][None], (group, most, width))

    def chunk(c, carry):
        for e in range(CHUNK):
            picked[pl.ds(e, 1), :] = table[pl.ds(rows_ref[c * CHUNK + e], 1), :]
        halo = picked[...].reshape(group, slots, width)
        both = jnp.concatenate([halo, hubs], axis=1)
        send_ref[pl.ds(c * group, group), :, :] = both.astype(BF16)
        return carry

    lax.fori_loop(0, rows_ref.shape[0] // CHUNK, chunk, 0)


def window_of(starts_ref, c, last_chunk, last_row):
    low = (starts_ref[0, c] // 16) * 16
    until = starts_ref[0, jnp.minimum(c + 1, last_chunk)]
    until = jnp.where(c < last_chunk, until, last_row)
    return low, (until - low) // WINDOW + 1


def targets_of(dst_ref, c, count):
    lane = lax.broadcasted_iota(jnp.int32, (1, CHUNK), 1)
    row = dst_ref[:, pl.ds(pl.multiple_of(c * CHUNK, CHUNK), CHUNK)]
    return jnp.where(lane + c * CHUNK < count, row, -1)


def one_hot(row, at):
    row_id = lax.broadcasted_iota(jnp.int32, (WINDOW, CHUNK), 0)
    return jnp.where(row_id + at == row, 1.0, 0.0).astype(BF16)


def forward_kernel(
    count_ref, starts_ref, src_ref, ids_ref, dst_ref, from_ref, feats_ref, come_ref, cot_ref, self_ref,
    neigh_ref, bias_ref, out_ref, own_ref, spread_ref, send_ref, table, come, picked_a, picked_b, sums,
    hub_counts, hub_grads, weights_ref, wgrad,
):
    local_rows, width = feats_ref.shape
    wide = self_ref.shape[1]
    peers, depth, _ = come_ref.shape
    slots = depth - HUB_MOST
    halo_rows = peers * slots
    hub_total = ids_ref.shape[0]
    hub_wide = hub_counts.shape[1]
    hub_base = local_rows + halo_rows
    last_chunk = dst_ref.shape[1] // CHUNK - 1
    count = count_ref[0]
    pairs = (count + (2 * CHUNK - 1)) // (2 * CHUNK)

    table[0:local_rows, :] = feats_ref[...].astype(F32)
    come[...] = come_ref[...].astype(F32).reshape(peers * depth, width)
    table[local_rows:hub_base, :] = (
        come[...].reshape(peers, depth, width)[:, 0:slots, :].reshape(halo_rows, width)
    )
    before, offset = jnp.int32(-1), jnp.int32(0)
    for h in range(hub_total):
        owner = ids_ref[h] // local_rows
        offset = jnp.where(owner == before, offset + 1, 0)
        before = owner
        table[pl.ds(hub_base + h, 1), :] = come[pl.ds(owner * depth + slots + offset, 1), :]
    sums[...] = jnp.zeros_like(sums)
    hub_counts[...] = jnp.zeros_like(hub_counts)
    hub_id = lax.broadcasted_iota(jnp.int32, (hub_wide, CHUNK), 0) + hub_base

    def gather(c, into):
        for e in range(CHUNK):
            into[pl.ds(e, 1), :] = table[pl.ds(src_ref[c * CHUNK + e], 1), :]

    def add_up(c, held):
        low, blocks = window_of(starts_ref, c, last_chunk, local_rows - 1)
        row = targets_of(dst_ref, c, count)
        source = from_ref[:, pl.ds(pl.multiple_of(c * CHUNK, CHUNK), CHUNK)]
        hub_hot = jnp.where(hub_id == source, 1.0, 0.0).astype(BF16)
        rhs = jnp.concatenate([held[...].astype(BF16), jnp.ones((CHUNK, width), BF16)], axis=1)

        def block(i):
            at = pl.multiple_of(low + i * WINDOW, 16)
            hot = one_hot(row, at)
            sums[pl.ds(at, WINDOW), :] += jnp.dot(hot, rhs, preferred_element_type=F32)
            hub_counts[pl.ds(at, WINDOW), :] += lax.dot_general(
                hot, hub_hot, (((1,), (1,)), ((), ())), preferred_element_type=F32
            )

        block(0)

        def step(i, inner):
            block(i)
            return inner

        lax.fori_loop(1, blocks, step, 0)

    def forward(p, carry):
        for half, held, ahead in ((0, picked_a, picked_b), (1, picked_b, picked_a)):
            c = 2 * p + half
            gather(jnp.minimum(c + 1, last_chunk), ahead)
            add_up(c, held)
        return carry

    gather(0, picked_a)
    lax.fori_loop(0, pairs, forward, 0)

    wgrad[...] = jnp.zeros_like(wgrad)
    hub_grads[...] = jnp.zeros_like(hub_grads)
    weights_ref[0:width, :] = self_ref[...]
    weights_ref[width:, :] = neigh_ref[...]
    bias = bias_ref[...]

    def dense(b, bias_sum):
        at = pl.multiple_of(b * CHUNK, CHUNK)
        weights = weights_ref[...]
        inverse = 1.0 / jnp.maximum(sums[pl.ds(at, CHUNK), width:], 1.0)
        mean = (sums[pl.ds(at, CHUNK), :width] * inverse).astype(BF16)
        both = jnp.concatenate([feats_ref[pl.ds(at, CHUNK), :], mean], axis=1)
        linear = jnp.dot(both, weights, preferred_element_type=F32) + bias
        logistic = jax.nn.sigmoid(linear)
        out_ref[pl.ds(at, CHUNK), :] = (linear * logistic).astype(BF16)
        slope = logistic * (1.0 + linear * (1.0 - logistic))
        grad = (cot_ref[pl.ds(at, CHUNK), :].astype(F32) * slope).astype(BF16)
        wgrad[...] += lax.dot_general(both, grad, (((0,), (0,)), ((), ())), preferred_element_type=F32)
        back = lax.dot_general(grad, weights, (((1,), (1,)), ((), ())), preferred_element_type=F32)
        own_ref[pl.ds(at, CHUNK), :] = back[:, :width]
        spread = (back[:, width:] * inverse).astype(BF16)
        spread_ref[pl.ds(at, CHUNK), :] = spread
        hub_grads[...] += lax.dot_general(
            hub_counts[pl.ds(at, CHUNK), :].astype(BF16), spread, (((0,), (0,)), ((), ())),
            preferred_element_type=F32,
        )
        return bias_sum + jnp.sum(grad.astype(F32), axis=0, keepdims=True)

    bias_sum = lax.fori_loop(0, local_rows // CHUNK, dense, jnp.zeros((1, wide), F32))

    come[...] = jnp.zeros_like(come)
    before, offset = jnp.int32(-1), jnp.int32(0)
    for h in range(hub_total):
        owner = ids_ref[h] // local_rows
        offset = jnp.where(owner == before, offset + 1, 0)
        before = owner
        come[pl.ds(owner * depth + offset, 1), :] = hub_grads[pl.ds(h, 1), :]
    for j in range(2):
        for k, value in ((0, wgrad[:, j * width : (j + 1) * width]), (4, bias_sum[:, j * width : (j + 1) * width])):
            high = value.astype(BF16).astype(F32)
            at = HUB_MOST + k + j
            come[pl.ds(at, peers, stride=depth), :] = jnp.broadcast_to(high, (peers, width))
            come[pl.ds(at + 2, peers, stride=depth), :] = jnp.broadcast_to(value - high, (peers, width))
    group = CHUNK // depth

    def emit(b, carry):
        at = pl.multiple_of(b * CHUNK, CHUNK)
        send_ref[pl.ds(b * group, group), :, :] = (
            come[pl.ds(at, CHUNK), :].reshape(group, depth, width).astype(BF16)
        )
        return carry

    lax.fori_loop(0, peers * depth // CHUNK, emit, 0)


def backward_kernel(
    count_ref, starts_ref, src_ref, dst_ref, spread_ref, own_ref, sum_ref, send_ref, spread, picked_a,
    picked_b, *accs,
):
    local_rows, width = own_ref.shape
    peers, slots, _ = send_ref.shape
    halo_rows = peers * slots
    last_chunk = dst_ref.shape[1] // CHUNK - 1
    count = count_ref[0]
    pairs = (count + (2 * CHUNK - 1)) // (2 * CHUNK)
    spread[0:local_rows, :] = spread_ref[...]
    spread[pl.ds(local_rows, WINDOW), :] = jnp.zeros((WINDOW, width), BF16)
    for acc in accs:
        acc[...] = jnp.zeros_like(acc)

    def expand(c, into):
        low, blocks = window_of(starts_ref, c, last_chunk, local_rows - 1)
        row = targets_of(dst_ref, c, count)

        def block(i):
            at = pl.multiple_of(low + i * WINDOW, 16)
            return lax.dot_general(
                one_hot(row, at), spread[pl.ds(at, WINDOW), :], (((0,), (0,)), ((), ())),
                preferred_element_type=F32,
            )

        into[...] = block(0)

        def step(i, inner):
            into[...] += block(i)
            return inner

        lax.fori_loop(1, blocks, step, 0)

    def scatter(c, held):
        for e in range(0, CHUNK, ACCS):
            to = [src_ref[c * CHUNK + e + k] for k in range(ACCS)]
            new = [accs[k][pl.ds(to[k], 1), :] + held[pl.ds(e + k, 1), :] for k in range(ACCS)]
            for k in range(ACCS):
                accs[k][pl.ds(to[k], 1), :] = new[k]

    def backward(p, carry):
        for half, held, ahead in ((0, picked_a, picked_b), (1, picked_b, picked_a)):
            c = 2 * p + half
            scatter(c, held)
            expand(jnp.minimum(c + 1, last_chunk), ahead)
        return carry

    expand(0, picked_a)
    lax.fori_loop(0, pairs, backward, 0)

    def total(at, size):
        value = accs[0][pl.ds(at, size), :]
        for acc in accs[1:]:
            value = value + acc[pl.ds(at, size), :]
        return value

    group = CHUNK // slots

    def fold(b, carry):
        at = pl.multiple_of(b * CHUNK, CHUNK)
        sum_ref[pl.ds(at, CHUNK), :] = own_ref[pl.ds(at, CHUNK), :] + total(at, CHUNK)
        return carry

    def emit(b, carry):
        at = pl.multiple_of(local_rows + b * CHUNK, CHUNK)
        send_ref[pl.ds(b * group, group), :, :] = (
            total(at, CHUNK).reshape(group, slots, width).astype(BF16)
        )
        return carry

    lax.fori_loop(0, local_rows // CHUNK, fold, 0)
    lax.fori_loop(0, halo_rows // CHUNK, emit, 0)


def finish_kernel(own_index_ref, ids_ref, rows_ref, own_ref, back_ref, hubs_ref, grad_ref, rows_in, *accs):
    local_rows, width = own_ref.shape
    peers, slots, _ = back_ref.shape
    accs[0][...] = own_ref[...]
    for acc in accs[1:]:
        acc[...] = jnp.zeros_like(acc)
    rows_in[...] = back_ref[...].astype(F32).reshape(peers * slots, width)

    def chunk(c, carry):
        at = c * CHUNK
        for e in range(0, CHUNK, ACCS):
            to = [rows_ref[at + e + k] for k in range(ACCS)]
            new = [
                accs[k][pl.ds(to[k], 1), :] + rows_in[pl.ds(at + e + k, 1), :]
                for k in range(ACCS)
            ]
            for k in range(ACCS):
                accs[k][pl.ds(to[k], 1), :] = new[k]
        return carry

    lax.fori_loop(0, rows_ref.shape[0] // CHUNK, chunk, 0)
    floor = own_index_ref[0] * local_rows
    first = first_hub(ids_ref, floor)
    for i in range(HUB_MOST):
        held, to = own_hub(ids_ref, first, floor, local_rows, i)
        accs[0][pl.ds(to, 1), :] += jnp.where(held, hubs_ref[pl.ds(i, 1), :], 0.0)

    def fold(b, carry):
        at = pl.multiple_of(b * CHUNK, CHUNK)
        value = accs[0][pl.ds(at, CHUNK), :]
        for acc in accs[1:]:
            value = value + acc[pl.ds(at, CHUNK), :]
        grad_ref[pl.ds(at, CHUNK), :] = value.astype(BF16)
        return carry

    lax.fori_loop(0, local_rows // CHUNK, fold, 0)


def exchange(array):
    return lax.all_to_all(array, "vert", split_axis=0, concat_axis=0, tiled=True)


def body(
    feats, w_self, w_neigh, bias, cotangent, send_rows, hub_ids, edge_src, edge_dst, edge_count
):
    local_rows, width = feats.shape
    wide = w_self.shape[1]
    peers = lax.axis_size("vert")
    slots = send_rows.shape[2]
    hubs = hub_ids.shape[0]
    edges = edge_src.shape[1]
    halo_rows = peers * slots
    table_rows = -(-(local_rows + halo_rows + hubs) // 16) * 16
    own = lax.axis_index("vert").astype(jnp.int32).reshape(1)
    rows = send_rows.reshape(halo_rows)

    sent = pl.pallas_call(
        pack_kernel,
        out_shape=jax.ShapeDtypeStruct((peers, slots + HUB_MOST, width), BF16),
        in_specs=[SMEM, SMEM, SMEM, VMEM],
        out_specs=VMEM,
        scratch_shapes=[pltpu.VMEM((local_rows, width), F32), pltpu.VMEM((CHUNK, width), F32)],
        name="pack",
    )(own, hub_ids, rows, feats)
    come = exchange(sent)

    starts = edge_dst[:, ::CHUNK]
    vmem = pltpu.CompilerParams(vmem_limit_bytes=56 * 1024 * 1024)
    source = edge_src.reshape(edges)
    depth = slots + HUB_MOST
    hub_wide = -(-hubs // 128) * 128
    output, own_grad, spread, items = pl.pallas_call(
        forward_kernel,
        out_shape=(
            jax.ShapeDtypeStruct((local_rows, wide), BF16),
            jax.ShapeDtypeStruct((local_rows, width), F32),
            jax.ShapeDtypeStruct((local_rows, width), BF16),
            jax.ShapeDtypeStruct((peers, depth, width), BF16),
        ),
        in_specs=[SMEM, SMEM, SMEM, SMEM] + [VMEM] * 8,
        out_specs=(VMEM,) * 4,
        scratch_shapes=[
            pltpu.VMEM((table_rows, width), F32),
            pltpu.VMEM((peers * depth, width), F32),
            pltpu.VMEM((CHUNK, width), F32),
            pltpu.VMEM((CHUNK, width), F32),
            pltpu.VMEM((local_rows + 4 * WINDOW, 2 * width), F32),
            pltpu.VMEM((local_rows + 4 * WINDOW, hub_wide), F32),
            pltpu.VMEM((hub_wide, width), F32),
            pltpu.VMEM((2 * width, wide), BF16),
            pltpu.VMEM((2 * width, wide), F32),
        ],
        compiler_params=vmem,
        name="forward",
    )(
        edge_count, starts, source, hub_ids, edge_dst, edge_src, feats, come, cotangent,
        w_self, w_neigh, bias.reshape(1, wide),
    )
    items = exchange(items)
    own_grad, outgoing = pl.pallas_call(
        backward_kernel,
        out_shape=(
            jax.ShapeDtypeStruct((local_rows, width), F32),
            jax.ShapeDtypeStruct((peers, slots, width), BF16),
        ),
        in_specs=[SMEM, SMEM, SMEM] + [VMEM] * 3,
        out_specs=(VMEM, VMEM),
        scratch_shapes=[
            pltpu.VMEM((local_rows + WINDOW, width), BF16),
            pltpu.VMEM((CHUNK, width), F32),
            pltpu.VMEM((CHUNK, width), F32),
        ]
        + [pltpu.VMEM((table_rows, width), F32)] * ACCS,
        compiler_params=vmem,
        name="backward",
    )(edge_count, starts, source, edge_dst, spread, own_grad)
    back = exchange(outgoing)
    summed = jnp.sum(items.astype(F32), axis=0)
    at = HUB_MOST
    mine = (summed[at : at + 2] + summed[at + 2 : at + 4])[None]
    grad_bias = (summed[at + 4 : at + 6] + summed[at + 6 : at + 8]).reshape(wide)
    shared = exchange(jnp.broadcast_to(mine, (peers, 2, width)))
    grad_feats = pl.pallas_call(
        finish_kernel,
        out_shape=jax.ShapeDtypeStruct((local_rows, width), BF16),
        in_specs=[SMEM, SMEM, SMEM] + [VMEM] * 3,
        out_specs=VMEM,
        scratch_shapes=[pltpu.VMEM((halo_rows, width), F32)]
        + [pltpu.VMEM((local_rows, width), F32)] * ACCS,
        name="finish",
    )(own, hub_ids, rows, own_grad, back, summed[:HUB_MOST])
    shared = shared.reshape(2 * width, wide)
    return (output, grad_feats, shared[:width], shared[width:], grad_bias)


def solution(mesh):
    in_specs = (
        P("vert", None),
        P(),
        P(),
        P(),
        P("vert", None),
        P("vert", None, None),
        P(),
        P("vert", None),
        P("vert", None),
        P("vert"),
    )
    out_specs = (P("vert", None), P("vert", None), P(), P(), P())
    return jax.shard_map(body, mesh=mesh, in_specs=in_specs, out_specs=out_specs, check_vma=False)
```

time: 181 us -> 184 us (1.017)
  blocking collectives: 74.5 us -> 0 us
  starting transfers between devices: 20.4 us -> 58.2 us
  waiting for transfers between devices: 48 us -> 80 us
  Pallas kernels: 28.2 us -> 35.4 us
    all_to_all x1 -> x0, blocking collectives: 74.5 us -> none  [exchange(): lax.all_to_all(array, 'vert', split_axis=0, concat_axis=0, tiled=True)]
    all_to_all x2 -> x4, starting transfers between devices: 20.4 us -> 58.2 us  [exchange(): lax.all_to_all(array, 'vert', split_axis=0, concat_axis=0, tiled=True)]
    all_to_all x2 -> x4, waiting for transfers between devices: 48 us -> 80 us  [exchange(): lax.all_to_all(array, 'vert', split_axis=0, concat_axis=0, tiled=True)]
    pallas_call x2 -> x3, Pallas kernels: 24.3 us -> 31.5 us  [the longest x1 18 us: body(): pl.pallas_call(forward_kernel, out_shape=(jax.ShapeDtypeStruct((local_row...]
  transfers between devices with their start and end apart: 2 -> 4, of which waited for: 2 -> 4; matrix products, arithmetic and copies ran while one was open for 1% -> 2% of each run, Pallas kernels for 0% -> 7%
where the time goes in v1:
time: 184 us; the launch traced here: 182 us
  waiting for transfers between devices  80 us (43%)
  starting transfers between devices  58.2 us (32%)
  Pallas kernels  35.4 us (19%)
  local copies, waits for them, and re-layouts  6.21 us (3%)
    all_to_all x4, waiting for transfers between devices, exchange(): lax.all_to_all(array, 'vert', split_axis=0, concat_axis=0, tiled=True)  80 us
    all_to_all x4, starting transfers between devices, exchange(): lax.all_to_all(array, 'vert', split_axis=0, concat_axis=0, tiled=True)  58.2 us
    pallas_call x1, Pallas kernels, body(): pl.pallas_call(forward_kernel, out_shape=(jax.ShapeDtypeStruct((local_row...  18 us
    pallas_call x1, Pallas kernels, body(): pl.pallas_call(backward_kernel, out_shape=(jax.ShapeDtypeStruct((local_ro...  8.44 us
    pallas_call x1, Pallas kernels, body(): pl.pallas_call(finish_kernel, out_shape=jax.ShapeDtypeStruct((local_rows,...  5.06 us
    pallas_call x1, Pallas kernels, body(): pl.pallas_call(pack_kernel, out_shape=jax.ShapeDtypeStruct((peers, slots...  3.94 us
  transfers between devices with their start and end apart: 4, of which 4 were waited for; matrix products, arithmetic and copies ran while one was open for 2% of the time, Pallas kernels for 7%

profile of v1, /device:TPU:2, one launch (start us, length us, event | category | flops | bytes accessed | tf_op | source)
XLA Modules:
  0.0 182.1 jit_solution(15743748562818880599)
XLA Ops:
  0.6 0.8 copy.15
  1.5 0.7 reshape.31.rows_ref
  2.2 3.9 %pack.1 = bf16[256,16,128]{2,1,0:T(8,128)(2,1)} custom-call(s32[1]{0:T(128)} %bitcast.1.own_ref.own_index_ref, s32[368]{0:T(512)} %ids_ref.5, s32[2048]{0:T(1024)} %reshape.31.rows_ref, bf16[2048,128]{1,0:T(8,128)(2,1)} %feats_ref.3), custom_call_target="tpu_custom_call" | custom-call | tf_op jit(solution)/shard_map/pack/pallas_call | solution.py:337
  6.1 14.7 %all-to-all-start = ((bf16[256,16,128]{2,1,0:T(8,128)(2,1)}), bf16[256,16,128]{2,1,0:T(8,128)(2,1)S(1)}, u32[]{:S(2)}, u32[]{:S(2)}) async-start(bf16[256,16,128]{2,1,0:T(8,128)(2,1)} %pack.1), calls=%async_computation | async-start | bytes 2097152 | tf_op jit(solution)/shard_map/all_to_all | solution.py:320
  21.5 1.5 slice.30.starts_ref
  23.0 29.1 %all-to-all-done.come_ref = bf16[256,16,128]{2,1,0:T(8,128)(2,1)S(1)} async-done(((bf16[256,16,128]{2,1,0:T(8,128)(2,1)}), bf16[256,16,128]{2,1,0:T(8,128)(2,1)S(1)}, u32[]{:S(2)}, u32[]{:S(2)}) %all-to-all-start) | async-done | bytes 1048608 | tf_op jit(solution)/shard_map/all_to_all | solution.py:320
  52.1 0.0 copy-start
  52.1 1.0 copy-done
  53.1 18.0 %forward.1 = (bf16[2048,256]{1,0:T(8,128)(2,1)}, f32[2048,128]{1,0:T(8,128)}, bf16[2048,128]{1,0:T(8,128)(2,1)}, bf16[256,16,128]{2,1,0:T(8,128)(2,1)}) custom-call(s32[1]{0:T(128)S(6)} %copy.20.count_ref, s32[1,64]{1,0:T(1,128)} %slice.30.starts_ref, s32[16384]{0:T(1024)} %bitcast.11, s32[368]{0:T(512)} %ids_ref.5, s32[1,16384]{1,0:T(1,128)} %dst_ref.3, ...), custom_call_target="tpu_custom_call" | custom-call | tf_op jit(solution)/shard_map/forward/pallas_call | solution.py:352
  71.0 30.2 %all-to-all-start.2 = ((bf16[256,16,128]{2,1,0:T(8,128)(2,1)}), bf16[256,16,128]{2,1,0:T(8,128)(2,1)S(1)}, u32[]{:S(2)}, u32[]{:S(2)}) async-start(bf16[256,16,128]{2,1,0:T(8,128)(2,1)} %get-tuple-element.16), calls=%async_computation.2 | async-start | bytes 2097152 | tf_op jit(solution)/shard_map/all_to_all | solution.py:320
  101.2 8.4 %backward.1 = (f32[2048,128]{1,0:T(8,128)}, bf16[256,8,128]{2,1,0:T(8,128)(2,1)}) custom-call(s32[1]{0:T(128)S(6)} %copy.20.count_ref, s32[1,64]{1,0:T(1,128)} %slice.30.starts_ref, s32[16384]{0:T(1024)} %bitcast.12, s32[1,16384]{1,0:T(1,128)} %dst_ref.3, bf16[2048,128]{1,0:T(8,128)(2,1)} %get-tuple-element.12.spread_ref, f32[2048,128]{1,0:T(8,128)} %get-tuple-element.13.own_ref), custom_call_target="tpu_custom_call" | custom-call | tf_op jit(solution)/shard_map/backward/pallas_call | solution.py:380
  109.7 22.8 %all-to-all-done.2 = bf16[256,16,128]{2,1,0:T(8,128)(2,1)S(1)} async-done(((bf16[256,16,128]{2,1,0:T(8,128)(2,1)}), bf16[256,16,128]{2,1,0:T(8,128)(2,1)S(1)}, u32[]{:S(2)}, u32[]{:S(2)}) %all-to-all-start.2) | async-done | bytes 1048608 | tf_op jit(solution)/shard_map/all_to_all | solution.py:320
  132.5 7.3 %all-to-all-start.1 = ((bf16[256,8,128]{2,1,0:T(8,128)(2,1)}), bf16[256,8,128]{2,1,0:T(8,128)(2,1)S(1)}, u32[]{:S(2)}, u32[]{:S(2)}) async-start(bf16[256,8,128]{2,1,0:T(8,128)(2,1)} %get-tuple-element.15), calls=%async_computation.1 | async-start | bytes 1048576 | tf_op jit(solution)/shard_map/all_to_all | solution.py:320
  139.9 0.3 convert_reduce_fusion
  140.2 0.6 fusion
  140.7 19.2 %all-to-all-done.1.back_ref = bf16[256,8,128]{2,1,0:T(8,128)(2,1)S(1)} async-done(((bf16[256,8,128]{2,1,0:T(8,128)(2,1)}), bf16[256,8,128]{2,1,0:T(8,128)(2,1)S(1)}, u32[]{:S(2)}, u32[]{:S(2)}) %all-to-all-start.1) | async-done | bytes 524320 | tf_op jit(solution)/shard_map/all_to_all | solution.py:320
  160.0 0.0 copy-start.1
  160.0 0.9 broadcast_in_dim.2
  160.8 6.0 %all-to-all-start.3 = ((f32[256,2,128]{2,1,0:T(2,128)}), f32[256,2,128]{2,1,0:T(2,128)S(1)}, u32[]{:S(2)}, u32[]{:S(2)}) async-start(f32[256,2,128]{2,1,0:T(2,128)} %broadcast_in_dim.2), calls=%async_computation.3 | async-start | bytes 524288 | tf_op jit(solution)/shard_map/all_to_all | solution.py:320
  166.8 0.6 slice.40.hubs_ref
  167.4 0.0 copy-done.1
  167.4 5.1 %finish.1 = bf16[2048,128]{1,0:T(8,128)(2,1)} custom-call(s32[1]{0:T(128)} %bitcast.1.own_ref.own_index_ref, s32[368]{0:T(512)} %ids_ref.5, s32[2048]{0:T(1024)} %reshape.31.rows_ref, f32[2048,128]{1,0:T(8,128)} %get-tuple-element.14.own_ref, bf16[256,8,128]{2,1,0:T(8,128)(2,1)} %copy-done.1, f32[8,128]{1,0:T(8,128)} %slice.40.hubs_ref), custom_call_target="tpu_custom_call" | custom-call | tf_op jit(solution)/shard_map/finish/pallas_call | solution.py:403
  172.5 8.8 %all-to-all-done.3 = f32[256,2,128]{2,1,0:T(2,128)S(1)} async-done(((f32[256,2,128]{2,1,0:T(2,128)}), f32[256,2,128]{2,1,0:T(2,128)S(1)}, u32[]{:S(2)}, u32[]{:S(2)}) %all-to-all-start.3) | async-done | bytes 262176 | tf_op jit(solution)/shard_map/all_to_all | solution.py:320
  181.4 0.7 copy_bitcast_fusion
  (1 shorter events, 0.0 us)
Async XLA Ops:
  6.1 46.0 %all-to-all-start = ((bf16[256,16,128]{2,1,0:T(8,128)(2,1)}), bf16[256,16,128]{2,1,0:T(8,128)(2,1)S(1)}, u32[]{:S(2)}, u32[]{:S(2)}) async-start(bf16[256,16,128]{2,1,0:T(8,128)(2,1)} %pack.1), calls=%async_computation | async-start | bytes 2097152 | tf_op jit(solution)/shard_map/all_to_all | solution.py:320
  52.1 1.0 copy-start
  71.0 61.5 %all-to-all-start.2 = ((bf16[256,16,128]{2,1,0:T(8,128)(2,1)}), bf16[256,16,128]{2,1,0:T(8,128)(2,1)S(1)}, u32[]{:S(2)}, u32[]{:S(2)}) async-start(bf16[256,16,128]{2,1,0:T(8,128)(2,1)} %get-tuple-element.16), calls=%async_computation.2 | async-start | bytes 2097152 | tf_op jit(solution)/shard_map/all_to_all | solution.py:320
  132.5 27.4 %all-to-all-start.1 = ((bf16[256,8,128]{2,1,0:T(8,128)(2,1)}), bf16[256,8,128]{2,1,0:T(8,128)(2,1)S(1)}, u32[]{:S(2)}, u32[]{:S(2)}) async-start(bf16[256,8,128]{2,1,0:T(8,128)(2,1)} %get-tuple-element.15), calls=%async_computation.1 | async-start | bytes 1048576 | tf_op jit(solution)/shard_map/all_to_all | solution.py:320
  160.0 7.5 %copy-start.1 = (bf16[256,8,128]{2,1,0:T(8,128)(2,1)}, bf16[256,8,128]{2,1,0:T(8,128)(2,1)S(1)}, u32[]{:S(2)}) copy-start(bf16[256,8,128]{2,1,0:T(8,128)(2,1)S(1)} %all-to-all-done.1.back_ref) | copy-start | bytes 1572868
  160.8 20.5 %all-to-all-start.3 = ((f32[256,2,128]{2,1,0:T(2,128)}), f32[256,2,128]{2,1,0:T(2,128)S(1)}, u32[]{:S(2)}, u32[]{:S(2)}) async-start(f32[256,2,128]{2,1,0:T(2,128)} %broadcast_in_dim.2), calls=%async_computation.3 | async-start | bytes 524288 | tf_op jit(solution)/shard_map/all_to_all | solution.py:320

commit v2 on v0

--- a/solution.py
+++ b/solution.py
@@ -245,14 +245,10 @@
     lax.fori_loop(0, halo_rows // CHUNK, emit, 0)
 
 
-def finish_kernel(
-    floor_ref, shifted_ref, ids_ref, rows_ref, own_ref, back_ref, items_ref, grad_ref, self_ref, neigh_ref,
-    bias_ref, rows_in, *accs,
-):
+def collect_kernel(rows_ref, own_ref, back_ref, sum_ref, rows_in, *accs):
     local_rows, width = own_ref.shape
     peers, _, _ = back_ref.shape
     slots = rows_ref.shape[0] // peers
-    half = self_ref.shape[0]
     accs[0][...] = own_ref[...]
     for acc in accs[1:]:
         acc[...] = jnp.zeros_like(acc)
@@ -271,30 +267,40 @@
         return carry
 
     lax.fori_loop(0, rows_ref.shape[0] // CHUNK, chunk, 0)
-    floor = floor_ref[0]
-    first = first_hub(shifted_ref, 0)
-    for i in range(HUB_MOST):
-        held, to = own_hub(ids_ref, first, floor, local_rows, i)
-        item = jnp.where(held, 4 * half + 8 + first + i, 0)
-        row = items_ref[pl.ds((item % peers) * ITEMS + item // peers, 1), :]
-        row = jnp.where(held, row, 0.0)
-        accs[0][pl.ds(to, 1), :] += row
 
     def fold(b, carry):
         at = pl.multiple_of(b * CHUNK, CHUNK)
         value = accs[0][pl.ds(at, CHUNK), :]
         for acc in accs[1:]:
             value = value + acc[pl.ds(at, CHUNK), :]
-        grad_ref[pl.ds(at, CHUNK), :] = value.astype(BF16)
+        sum_ref[pl.ds(at, CHUNK), :] = value
         return carry
 
     lax.fori_loop(0, local_rows // CHUNK, fold, 0)
+
+
+def finish_kernel(
+    floor_ref, ids_ref, sum_ref, share_ref, grad_ref, self_ref, neigh_ref, bias_ref, total, items,
+):
+    local_rows, width = sum_ref.shape
+    peers = share_ref.shape[0] // ITEMS
+    half = self_ref.shape[0]
+    total[...] = sum_ref[...]
+    items[...] = share_ref[...].astype(F32)
+    floor = floor_ref[0]
+    first = first_hub(ids_ref, floor)
+    for i in range(HUB_MOST):
+        held, to = own_hub(ids_ref, first, floor, local_rows, i)
+        item = jnp.where(held, 4 * half + 8 + first + i, 0)
+        row = items[pl.ds((item % peers) * ITEMS + item // peers, 1), :]
+        total[pl.ds(to, 1), :] += jnp.where(held, row, 0.0)
+    grad_ref[...] = total[...].astype(BF16)
     for j in range(2):
-        item = items_ref[pl.ds(j, peers, stride=ITEMS), :]
+        item = items[pl.ds(j, peers, stride=ITEMS), :]
         self_ref[:, j * width : (j + 1) * width] = item[:half]
         neigh_ref[:, j * width : (j + 1) * width] = item[half:]
     for j in range(2):
-        bias_ref[:, j * width : (j + 1) * width] = items_ref[pl.ds(j * ITEMS + 2, 1), :]
+        bias_ref[:, j * width : (j + 1) * width] = items[pl.ds(j * ITEMS + 2, 1), :]
 
 
 def exchange(array):
@@ -354,11 +360,19 @@
         w_self, w_neigh, bias.reshape(1, wide),
     )
     back = exchange(outgoing)
-    hubs_a = hub_ids - own * local_rows
     floors = lax.iota(jnp.int32, 8) + own * local_rows
     summed = jnp.sum(back[:, slots:].astype(F32), axis=0)
-    items = (summed[:ITEMS] + summed[ITEMS:])[None]
+    items = (summed[:ITEMS] + summed[ITEMS:]).astype(BF16)[None]
     items = exchange(jnp.broadcast_to(items, (peers, ITEMS, width)))
+    sums = pl.pallas_call(
+        collect_kernel,
+        out_shape=jax.ShapeDtypeStruct((local_rows, width), F32),
+        in_specs=[SMEM, VMEM, VMEM],
+        out_specs=VMEM,
+        scratch_shapes=[pltpu.VMEM((halo_rows, width), F32)]
+        + [pltpu.VMEM((local_rows, width), F32)] * ACCS,
+        name="collect",
+    )(rows, own_grad, back)
     grad_feats, grad_self, grad_neigh, grad_bias = pl.pallas_call(
         finish_kernel,
         out_shape=(
@@ -367,12 +381,14 @@
             jax.ShapeDtypeStruct((width, wide), F32),
             jax.ShapeDtypeStruct((1, wide), F32),
         ),
-        in_specs=[SMEM, SMEM, SMEM, SMEM] + [VMEM] * 3,
+        in_specs=[SMEM, SMEM, VMEM, VMEM],
         out_specs=(VMEM,) * 4,
-        scratch_shapes=[pltpu.VMEM((halo_rows, width), F32)]
-        + [pltpu.VMEM((local_rows, width), F32)] * ACCS,
+        scratch_shapes=[
+            pltpu.VMEM((local_rows, width), F32),
+            pltpu.VMEM((peers * ITEMS, width), F32),
+        ],
         name="finish",
-    )(floors, hubs_a, hub_ids, rows, own_grad, back, items.reshape(peers * ITEMS, width))
+    )(floors, hub_ids, sums, items.reshape(peers * ITEMS, width))
     return (output, grad_feats, grad_self, grad_neigh, grad_bias.reshape(wide))
 
 

time: 181 us -> 173 us (0.956)
  waiting for transfers between devices: 48 us -> 37.9 us
  Pallas kernels: 28.2 us -> 30.4 us
    all_to_all x2, waiting for transfers between devices: 48 us -> 37.9 us  [exchange(): lax.all_to_all(array, 'vert', split_axis=0, concat_axis=0, tiled=True)]
    pallas_call x0 -> x1, Pallas kernels: none -> 5.28 us  [body(): pl.pallas_call(collect_kernel, out_shape=jax.ShapeDtypeStruct((local_rows...]
    pallas_call x1, Pallas kernels: 5.47 us -> 2.37 us  [body(): pl.pallas_call(finish_kernel, out_shape=(jax.ShapeDtypeStruct((local_rows...]
  transfers between devices with their start and end apart: 2 -> 2, of which waited for: 2 -> 2; matrix products, arithmetic and copies ran while one was open for 1% -> 1% of each run, Pallas kernels for 0% -> 3%
where the time goes in v2:
time: 173 us; the launch traced here: 171 us
  blocking collectives  74.5 us (43%)
  waiting for transfers between devices  37.9 us (22%)
  Pallas kernels  30.4 us (18%)
  starting transfers between devices  20.4 us (12%)
  local copies, waits for them, and re-layouts  5.59 us (3%)
    all_to_all x1, blocking collectives, exchange(): lax.all_to_all(array, 'vert', split_axis=0, concat_axis=0, tiled=True)  74.5 us
    all_to_all x2, waiting for transfers between devices, exchange(): lax.all_to_all(array, 'vert', split_axis=0, concat_axis=0, tiled=True)  37.9 us
    all_to_all x2, starting transfers between devices, exchange(): lax.all_to_all(array, 'vert', split_axis=0, concat_axis=0, tiled=True)  20.4 us
    pallas_call x1, Pallas kernels, body(): pl.pallas_call(layer_kernel, out_shape=(jax.ShapeDtypeStruct((local_rows,...  18.8 us
    pallas_call x1, Pallas kernels, body(): pl.pallas_call(collect_kernel, out_shape=jax.ShapeDtypeStruct((local_rows...  5.28 us
    pallas_call x1, Pallas kernels, body(): pl.pallas_call(pack_kernel, out_shape=jax.ShapeDtypeStruct((peers, slots...  3.94 us
  transfers between devices with their start and end apart: 2, of which 2 were waited for; matrix products, arithmetic and copies ran while one was open for 1% of the time, Pallas kernels for 3%

profile of v2, /device:TPU:2, one launch (start us, length us, event | category | flops | bytes accessed | tf_op | source)
XLA Modules:
  0.0 170.9 jit_solution(15651630170881363549)
XLA Ops:
  0.6 0.8 copy.15
  1.5 0.7 reshape.31.rows_ref
  2.2 3.9 %pack.1 = bf16[256,16,128]{2,1,0:T(8,128)(2,1)} custom-call(s32[1]{0:T(128)} %bitcast.1.own_ref, s32[368]{0:T(512)} %ids_ref.5, s32[2048]{0:T(1024)} %reshape.31.rows_ref, bf16[2048,128]{1,0:T(8,128)(2,1)} %feats_ref.3), custom_call_target="tpu_custom_call" | custom-call | tf_op jit(solution)/shard_map/pack/pallas_call | solution.py:324
  6.1 14.7 %all-to-all-start = ((bf16[256,16,128]{2,1,0:T(8,128)(2,1)}), bf16[256,16,128]{2,1,0:T(8,128)(2,1)S(1)}, u32[]{:S(2)}, u32[]{:S(2)}) async-start(bf16[256,16,128]{2,1,0:T(8,128)(2,1)} %pack.1), calls=%async_computation | async-start | bytes 2097152 | tf_op jit(solution)/shard_map/all_to_all | solution.py:307
  21.5 1.5 slice.12.starts_ref
  23.0 29.1 %all-to-all-done.come_ref = bf16[256,16,128]{2,1,0:T(8,128)(2,1)S(1)} async-done(((bf16[256,16,128]{2,1,0:T(8,128)(2,1)}), bf16[256,16,128]{2,1,0:T(8,128)(2,1)S(1)}, u32[]{:S(2)}, u32[]{:S(2)}) %all-to-all-start) | async-done | bytes 1048608 | tf_op jit(solution)/shard_map/all_to_all | solution.py:307
  52.1 0.0 copy-start.1
  52.1 1.0 copy-done.1
  53.1 18.8 %layer.1 = (bf16[2048,256]{1,0:T(8,128)(2,1)}, f32[2048,128]{1,0:T(8,128)}, bf16[256,16,128]{2,1,0:T(8,128)(2,1)}) custom-call(s32[1]{0:T(128)S(6)} %copy.16.count_ref, s32[1,64]{1,0:T(1,128)} %slice.12.starts_ref, s32[16384]{0:T(1024)} %bitcast.7, s32[368]{0:T(512)} %ids_ref.5, s32[1,16384]{1,0:T(1,128)} %dst_ref.1, bf16[2048,128]{1,0:T(8,128)(2,1)} %feats_ref.3, ...), custom_call_target="tpu_custom_call" | custom-call | tf_op jit(solution)/shard_map/layer/pallas_call | solution.py:335
  72.0 74.5 %all_to_all.15.back_ref = bf16[256,16,128]{2,1,0:T(8,128)(2,1)S(1)} all-to-all(bf16[256,16,128]{2,1,0:T(8,128)(2,1)} %get-tuple-element.14), channel_id=1, replica_groups=mesh['vert'=256] {'vert'}, dimensions={0} | all-to-all | bytes 2097152 | tf_op jit(solution)/shard_map/all_to_all | solution.py:307
  146.4 0.0 copy-start
  146.4 0.3 convert_reduce_fusion
  146.7 0.8 broadcast_in_dim.2
  147.5 5.7 %all-to-all-start.2 = ((bf16[256,4,128]{2,1,0:T(4,128)(2,1)}), bf16[256,4,128]{2,1,0:T(4,128)(2,1)S(1)}, u32[]{:S(2)}, u32[]{:S(2)}) async-start(bf16[256,4,128]{2,1,0:T(4,128)(2,1)} %broadcast_in_dim.2), calls=%async_computation.2 | async-start | bytes 524288 | tf_op jit(solution)/shard_map/all_to_all | solution.py:307
  153.3 0.5 iota_add_fusion.floor_ref
  153.8 0.0 copy-done
  153.8 5.3 %collect.1.sum_ref = f32[2048,128]{1,0:T(8,128)} custom-call(s32[2048]{0:T(1024)} %reshape.31.rows_ref, f32[2048,128]{1,0:T(8,128)} %get-tuple-element.13.own_ref, bf16[256,16,128]{2,1,0:T(8,128)(2,1)} %copy-done), custom_call_target="tpu_custom_call" | custom-call | tf_op jit(solution)/shard_map/collect/pallas_call | solution.py:367
  159.1 8.8 %all-to-all-done.2 = bf16[256,4,128]{2,1,0:T(4,128)(2,1)S(1)} async-done(((bf16[256,4,128]{2,1,0:T(4,128)(2,1)}), bf16[256,4,128]{2,1,0:T(4,128)(2,1)S(1)}, u32[]{:S(2)}, u32[]{:S(2)}) %all-to-all-start.2) | async-done | bytes 262176 | tf_op jit(solution)/shard_map/all_to_all | solution.py:307
  167.8 0.0 copy-start.2
  167.8 0.7 copy-done.2
  168.5 2.4 %finish.1 = (bf16[2048,128]{1,0:T(8,128)(2,1)}, f32[128,256]{1,0:T(8,128)}, f32[128,256]{1,0:T(8,128)}, f32[1,256]{1,0:T(1,128)}) custom-call(s32[8]{0:T(128)} %iota_add_fusion.floor_ref, s32[368]{0:T(512)} %ids_ref.5, f32[2048,128]{1,0:T(8,128)} %collect.1.sum_ref, bf16[1024,128]{1,0:T(8,128)(2,1)} %bitcast.6), custom_call_target="tpu_custom_call" | custom-call | tf_op jit(solution)/shard_map/finish/pallas_call | solution.py:376
  (1 shorter events, 0.0 us)
Async XLA Ops:
  6.1 46.0 %all-to-all-start = ((bf16[256,16,128]{2,1,0:T(8,128)(2,1)}), bf16[256,16,128]{2,1,0:T(8,128)(2,1)S(1)}, u32[]{:S(2)}, u32[]{:S(2)}) async-start(bf16[256,16,128]{2,1,0:T(8,128)(2,1)} %pack.1), calls=%async_computation | async-start | bytes 2097152 | tf_op jit(solution)/shard_map/all_to_all | solution.py:307
  52.1 1.0 copy-start.1
  146.4 7.4 %copy-start = (bf16[256,16,128]{2,1,0:T(8,128)(2,1)}, bf16[256,16,128]{2,1,0:T(8,128)(2,1)S(1)}, u32[]{:S(2)}) copy-start(bf16[256,16,128]{2,1,0:T(8,128)(2,1)S(1)} %all_to_all.15.back_ref) | copy-start | bytes 3145732
  147.5 20.3 %all-to-all-start.2 = ((bf16[256,4,128]{2,1,0:T(4,128)(2,1)}), bf16[256,4,128]{2,1,0:T(4,128)(2,1)S(1)}, u32[]{:S(2)}, u32[]{:S(2)}) async-start(bf16[256,4,128]{2,1,0:T(4,128)(2,1)} %broadcast_in_dim.2), calls=%async_computation.2 | async-start | bytes 524288 | tf_op jit(solution)/shard_map/all_to_all | solution.py:307
  167.8 0.7 copy-start.2
